TPU v7x, 32 devices: a whole 2x2x4 slice. The times are simulated.
32 devices in a mesh: dp: 8 (over z, y), mp: 4 (over x, core).
Axes of the slice: x: 2, y: 2, z: 4, core: 2. Of those that a mesh axis runs over, the one named last changes fastest.
Arguments:
- inputs: bfloat16 [8192, 768], P(('dp', 'mp')), may hold values from -6 to 6
- memory: bfloat16 [32768, 768], P(('dp', 'mp')), may hold values from -6 to 6
- target_len: int32 [64], P('dp'), may hold values from 8 to 114, as said below
- memory_len: int32 [64], P('dp'), may hold values from 32 to 512, as said below
- bucket_map: int32 [128], replicated, may hold values from 0 to 31, as said below
- self_gain: float32 [768], replicated, may hold values from 0.5 to 1.5
- self_query: bfloat16 [768, 768], P(None, 'mp'), may hold values from -0.02734375 to 0.02734375
- self_key: bfloat16 [768, 768], P(None, 'mp'), may hold values from -0.21875 to 0.21875
- self_value: bfloat16 [768, 768], P(None, 'mp'), may hold values from -0.21875 to 0.21875
- self_out: bfloat16 [768, 768], P('mp'), may hold values from -1.25 to 1.25
- bias_table: float32 [32, 12], P(None, 'mp'), may hold values from -4 to 4
- cross_gain: float32 [768], replicated, may hold values from 0.5 to 1.5
- cross_query: bfloat16 [768, 768], P(None, 'mp'), may hold values from -0.02734375 to 0.02734375
- cross_key: bfloat16 [768, 768], P(None, 'mp'), may hold values from -0.21875 to 0.21875
- cross_value: bfloat16 [768, 768], P(None, 'mp'), may hold values from -0.21875 to 0.21875
- cross_out: bfloat16 [768, 768], P('mp'), may hold values from -2.5 to 2.5
- feed_gain: float32 [768], replicated, may hold values from 0.5 to 1.5
- feed_input: bfloat16 [768, 3072], P(None, 'mp'), may hold values from -0.21875 to 0.21875
- feed_output: bfloat16 [3072, 768], P('mp'), may hold values from -0.15625 to 0.15625
- cotangent: bfloat16 [8192, 768], P(('dp', 'mp')), may hold values from -6 to 6
Outputs:
- layer_out: bfloat16 [8192, 768], P(('dp', 'mp'))
- inputs_grad: float32 [8192, 768], P(('dp', 'mp'))
- memory_grad: float32 [32768, 768], P(('dp', 'mp'))
- self_gain_grad: float32 [768], replicated
- self_query_grad: float32 [768, 768], P(None, 'mp')
- self_key_grad: float32 [768, 768], P(None, 'mp')
- self_value_grad: float32 [768, 768], P(None, 'mp')
- self_out_grad: float32 [768, 768], P('mp')
- bias_table_grad: float32 [32, 12], P(None, 'mp')
- cross_gain_grad: float32 [768], replicated
- cross_query_grad: float32 [768, 768], P(None, 'mp')
- cross_key_grad: float32 [768, 768], P(None, 'mp')
- cross_value_grad: float32 [768, 768], P(None, 'mp')
- cross_out_grad: float32 [768, 768], P('mp')
- feed_gain_grad: float32 [768], replicated
- feed_input_grad: float32 [768, 3072], P(None, 'mp')
- feed_output_grad: float32 [3072, 768], P('mp')
Inputs may be any that keep to these rules, and one draw needn't show every extreme that they name: bucket_map[d] is the bucket of a key d positions before its query: it equals d below 16, never falls as d grows, and reaches 31. An example's target rows at positions from target_len on are padding. An example's memory rows at positions from memory_len on are padding.
All inputs are finite; a program needn't handle non-finite values.
Results may differ from a plain program's by a relative error of at most 0.023.
Values may be sent and summed in bfloat16 or wider, within the bound.
No kernel may reach another device: no remote copies, remote signals or barrier semaphores. Data moves between devices by JAX's collectives and lax.ppermute only.
A program may use at most 128 MiB of HBM per device.

v0:
```python
import jax
import jax.numpy as jnp
from jax import lax
from jax.sharding import PartitionSpec as P

HEAD_DIM = 64
BUCKETS = 32
TGT_LEN = 128
MEM_LEN = 512
masked_fill = -1000000000.0
epsilon = 1e-06
highest = lax.Precision.HIGHEST
tanh_scale = 0.7978845608
cubic_term = 0.044715


def gelu_tanh(value):
    return 0.5 * value * (1.0 + jnp.tanh(tanh_scale * (value + cubic_term * value * value * value)))


def norm_forward(hidden, gain):
    scale = lax.rsqrt(jnp.mean(hidden * hidden, -1, keepdims=True) + epsilon)
    return (hidden * scale * gain, scale)


def norm_backward(hidden, scale, gain, upstream):
    weighted = gain * upstream
    return scale * weighted - hidden * scale**3 * jnp.mean(hidden * weighted, -1, keepdims=True)


def gather_normed(values):
    return lax.all_gather(values, "mp", axis=0, tiled=True)


def gather_upstream(values):
    return lax.all_gather(values, "mp", axis=0, tiled=True)


def project(rows, weight):
    return jnp.dot(rows, weight, preferred_element_type=jnp.float32).astype(jnp.bfloat16)


def back_project(grad_rows, weight):
    return lax.dot_general(
        grad_rows, weight, (((1,), (1,)), ((), ())), preferred_element_type=jnp.float32
    )


def weight_grad(rows, grad_rows):
    return jnp.einsum("rd,rc->dc", rows, grad_rows, preferred_element_type=jnp.float32)


def branch_sum(mixed, weight):
    return lax.psum_scatter(
        jnp.dot(mixed, weight, preferred_element_type=jnp.float32),
        "mp",
        scatter_dimension=0,
        tiled=True,
    )


def input_sum(weight_pairs, local_rows):
    summed = jnp.zeros((lax.axis_size("mp") * local_rows, weight_pairs[0][1].shape[0]), jnp.float32)
    for grad_rows, weight in weight_pairs:
        summed = summed + back_project(grad_rows, weight)
    return lax.psum_scatter(summed, "mp", scatter_dimension=0, tiled=True)


def split_heads(rows, groups, length):
    return rows.reshape(groups, length, rows.shape[1] // HEAD_DIM, HEAD_DIM)


def masked_scores(queries, key_blocks, extra, valid):
    scores = (
        jnp.einsum("eqhd,ekhd->ehqk", queries, key_blocks, preferred_element_type=jnp.float32)
        + extra
    )
    return jnp.where(valid, scores, masked_fill)


def attend(query_rows, key_rows, value_rows, extra, valid, key_len):
    groups = valid.shape[0]
    queries = split_heads(query_rows, groups, TGT_LEN)
    key_blocks = split_heads(key_rows, groups, key_len)
    value_blocks = split_heads(value_rows, groups, key_len)
    scores = masked_scores(queries, key_blocks, extra, valid)
    top_score = jnp.max(scores, -1, keepdims=True)
    log_total = top_score + jnp.log(jnp.sum(jnp.exp(scores - top_score), -1, keepdims=True))
    probs = jnp.exp(scores - log_total).astype(jnp.bfloat16)
    mixed = jnp.einsum("ehqk,ekhd->eqhd", probs, value_blocks, preferred_element_type=jnp.float32)
    return (mixed.astype(jnp.bfloat16).reshape(query_rows.shape), log_total)


def attend_back(query_rows, key_rows, value_rows, extra, valid, key_len, log_total, mixed_grad):
    groups = valid.shape[0]
    queries = split_heads(query_rows, groups, TGT_LEN)
    key_blocks = split_heads(key_rows, groups, key_len)
    value_blocks = split_heads(value_rows, groups, key_len)
    grad_blocks = split_heads(mixed_grad, groups, TGT_LEN)
    probs_full = jnp.exp(masked_scores(queries, key_blocks, extra, valid) - log_total)
    probs = probs_full.astype(jnp.bfloat16)
    value_grad = jnp.einsum(
        "ehqk,eqhd->ekhd", probs, grad_blocks, preferred_element_type=jnp.float32
    )
    prob_grad = jnp.einsum(
        "eqhd,ekhd->ehqk", grad_blocks, value_blocks, preferred_element_type=jnp.float32
    )
    score_grad = probs_full * (prob_grad - jnp.sum(probs_full * prob_grad, -1, keepdims=True))
    score_low = score_grad.astype(jnp.bfloat16)
    query_grad = jnp.einsum(
        "ehqk,ekhd->eqhd", score_low, key_blocks, preferred_element_type=jnp.float32
    )
    key_grad = jnp.einsum("ehqk,eqhd->ekhd", score_low, queries, preferred_element_type=jnp.float32)
    return (
        query_grad.astype(jnp.bfloat16).reshape(query_rows.shape),
        key_grad.astype(jnp.bfloat16).reshape(key_rows.shape),
        value_grad.astype(jnp.bfloat16).reshape(value_rows.shape),
        score_grad,
    )


def body(
    inputs,
    memory,
    target_len,
    memory_len,
    bucket_map,
    self_gain,
    self_query,
    self_key,
    self_value,
    self_out,
    bias_table,
    cross_gain,
    cross_query,
    cross_key,
    cross_value,
    cross_out,
    feed_gain,
    feed_input,
    feed_output,
    cotangent,
):
    local_rows = inputs.shape[0]
    positions = jnp.arange(TGT_LEN, dtype=jnp.int32)
    distance = jnp.maximum(positions[:, None] - positions[None, :], 0)
    lookup = distance[:, :, None] == positions[None, None, :]
    bucket_index = jnp.sum(jnp.where(lookup, bucket_map[None, None, :], 0), -1)
    causal = positions[None, :] <= positions[:, None]
    bucket_ids = jnp.arange(BUCKETS, dtype=jnp.int32)
    bucket_hot = (
        (bucket_index[:, :, None] == bucket_ids[None, None, :]) & causal[:, :, None]
    ).astype(jnp.float32)
    self_bias = jnp.einsum("qkb,bh->hqk", bucket_hot, bias_table, precision=highest)[None]
    self_valid = causal[None, None] & (
        positions[None, None, None, :] < target_len[:, None, None, None]
    )
    memory_pos = jnp.arange(MEM_LEN, dtype=jnp.int32)
    cross_valid = (memory_pos[None, :] < memory_len[:, None])[:, None, None, :]
    stream = inputs.astype(jnp.float32)
    normed_one, scale_one = norm_forward(stream, self_gain)
    gathered_one = gather_normed(normed_one.astype(jnp.bfloat16))
    self_queries = project(gathered_one, self_query)
    self_keys = project(gathered_one, self_key)
    self_values = project(gathered_one, self_value)
    self_mixed, self_total = attend(
        self_queries, self_keys, self_values, self_bias, self_valid, TGT_LEN
    )
    after_self = stream + branch_sum(self_mixed, self_out)
    normed_two, scale_two = norm_forward(after_self, cross_gain)
    gathered_two = gather_normed(normed_two.astype(jnp.bfloat16))
    memory_all = lax.all_gather(memory, "mp", axis=0, tiled=True)
    cross_queries = project(gathered_two, cross_query)
    cross_keys = project(memory_all, cross_key)
    cross_values = project(memory_all, cross_value)
    cross_mixed, cross_total = attend(
        cross_queries, cross_keys, cross_values, 0.0, cross_valid, MEM_LEN
    )
    after_cross = after_self + branch_sum(cross_mixed, cross_out)
    normed_three, scale_three = norm_forward(after_cross, feed_gain)
    gathered_three = gather_normed(normed_three.astype(jnp.bfloat16))
    pre_act = jnp.dot(gathered_three, feed_input, preferred_element_type=jnp.float32)
    act_value, act_pullback = jax.vjp(gelu_tanh, pre_act)
    activated = act_value.astype(jnp.bfloat16)
    result = after_cross + branch_sum(activated, feed_output)
    layer_out = result.astype(jnp.bfloat16)
    upstream = cotangent.astype(jnp.float32)
    feed_up = gather_upstream(cotangent)
    feed_output_part = weight_grad(activated, feed_up)
    hidden_grad = back_project(feed_up, feed_output)
    pre_grad = act_pullback(hidden_grad)[0].astype(jnp.bfloat16)
    feed_input_part = weight_grad(gathered_three, pre_grad)
    normed_three_grad = input_sum(((pre_grad, feed_input),), local_rows)
    feed_gain_part = jnp.sum(normed_three_grad * after_cross * scale_three, 0)
    grad_two = upstream + norm_backward(after_cross, scale_three, feed_gain, normed_three_grad)
    cross_up = gather_upstream(grad_two.astype(jnp.bfloat16))
    cross_out_part = weight_grad(cross_mixed, cross_up)
    mixed_two = back_project(cross_up, cross_out).astype(jnp.bfloat16)
    cross_q_grad, cross_k_grad, cross_v_grad, cross_score_grad = attend_back(
        cross_queries, cross_keys, cross_values, 0.0, cross_valid, MEM_LEN, cross_total, mixed_two
    )
    cross_query_part = weight_grad(gathered_two, cross_q_grad)
    cross_key_part = weight_grad(memory_all, cross_k_grad)
    cross_value_part = weight_grad(memory_all, cross_v_grad)
    late_totals = (
        cross_query_part,
        cross_key_part,
        cross_value_part,
        cross_out_part,
        feed_input_part,
        feed_output_part,
    )
    (
        cross_query_sum,
        cross_key_sum,
        cross_value_sum,
        cross_out_sum,
        feed_input_sum,
        feed_output_sum,
    ) = late_totals
    memory_grad = lax.psum_scatter(
        (back_project(cross_k_grad, cross_key) + back_project(cross_v_grad, cross_value)).astype(
            jnp.bfloat16
        ),
        "mp",
        scatter_dimension=0,
        tiled=True,
    ).astype(jnp.float32)
    normed_two_grad = input_sum(((cross_q_grad, cross_query),), local_rows)
    cross_gain_part = jnp.sum(normed_two_grad * after_self * scale_two, 0)
    grad_one = grad_two + norm_backward(after_self, scale_two, cross_gain, normed_two_grad)
    self_up = gather_upstream(grad_one.astype(jnp.bfloat16))
    self_out_part = weight_grad(self_mixed, self_up)
    mixed_one = back_project(self_up, self_out).astype(jnp.bfloat16)
    self_q_grad, self_k_grad, self_v_grad, self_score_grad = attend_back(
        self_queries, self_keys, self_values, self_bias, self_valid, TGT_LEN, self_total, mixed_one
    )
    bias_part = jnp.einsum("ehqk,qkb->bh", self_score_grad, bucket_hot, precision=highest)
    self_query_part = weight_grad(gathered_one, self_q_grad)
    self_key_part = weight_grad(gathered_one, self_k_grad)
    self_value_part = weight_grad(gathered_one, self_v_grad)
    normed_one_grad = input_sum(
        ((self_q_grad, self_query), (self_k_grad, self_key), (self_v_grad, self_value)), local_rows
    )
    self_gain_part = jnp.sum(normed_one_grad * stream * scale_one, 0)
    inputs_grad = grad_one + norm_backward(stream, scale_one, self_gain, normed_one_grad)
    gain_one, gain_two, gain_three = lax.psum(
        (self_gain_part, cross_gain_part, feed_gain_part), "mp"
    )
    every_total = lax.psum(
        (
            gain_one,
            self_query_part,
            self_key_part,
            self_value_part,
            self_out_part,
            bias_part,
            gain_two,
            cross_query_sum,
            cross_key_sum,
            cross_value_sum,
            cross_out_sum,
            gain_three,
            feed_input_sum,
            feed_output_sum,
        ),
        "dp",
    )
    (
        self_gain_sum,
        self_query_sum,
        self_key_sum,
        self_value_sum,
        self_out_sum,
        bias_sum,
        cross_gain_sum,
        cross_query_sum,
        cross_key_sum,
        cross_value_sum,
        cross_out_sum,
        feed_gain_sum,
        feed_input_sum,
        feed_output_sum,
    ) = every_total
    return (
        layer_out,
        inputs_grad,
        memory_grad,
        self_gain_sum,
        self_query_sum,
        self_key_sum,
        self_value_sum,
        self_out_sum,
        bias_sum,
        cross_gain_sum,
        cross_query_sum,
        cross_key_sum,
        cross_value_sum,
        cross_out_sum,
        feed_gain_sum,
        feed_input_sum,
        feed_output_sum,
    )


def solution(mesh):
    in_specs = (
        P(("dp", "mp"), None),
        P(("dp", "mp"), None),
        P("dp"),
        P("dp"),
        P(),
        P(),
        P(None, "mp"),
        P(None, "mp"),
        P(None, "mp"),
        P("mp", None),
        P(None, "mp"),
        P(),
        P(None, "mp"),
        P(None, "mp"),
        P(None, "mp"),
        P("mp", None),
        P(),
        P(None, "mp"),
        P("mp", None),
        P(("dp", "mp"), None),
    )
    out_specs = (
        P(("dp", "mp"), None),
        P(("dp", "mp"), None),
        P(("dp", "mp"), None),
        P(),
        P(None, "mp"),
        P(None, "mp"),
        P(None, "mp"),
        P("mp", None),
        P(None, "mp"),
        P(),
        P(None, "mp"),
        P(None, "mp"),
        P(None, "mp"),
        P("mp", None),
        P(),
        P(None, "mp"),
        P("mp", None),
    )
    return jax.shard_map(body, mesh=mesh, in_specs=in_specs, out_specs=out_specs, check_vma=False)
```

profile of v0, /device:TPU:0, one launch (start us, length us, event | category | flops | bytes accessed | tf_op | source)
XLA Modules:
  0.0 868.2 jit_solution(15124593207510473389)
XLA Ops:
  11.1 5.8 select_reduce_fusion
  17.6 2.4 copy.123
  21.8 11.7 %all-gather.8.cloned.1.call-done = bf16[1024,768]{1,0:T(8,128)(2,1)} async-done(((bf16[256,768]{1,0:T(8,128)(2,1)}), bf16[1024,768]{1,0:T(8,128)(2,1)}) %all-gather.8.cloned.1.call-update) | async-done | bytes 1572880 | tf_op jit(solution)/shard_map/all_gather | solution.py:32
  33.6 2.2 fusion.26
  39.9 2.3 fusion.75
  43.0 37.3 %reduce-scatter.8.cloned.1.call-done = f32[256,768]{1,0:T(8,128)} async-done(((f32[1024,768]{1,0:T(8,128)}), f32[256,768]{1,0:T(8,128)}) %reduce-scatter.8.cloned.1.call-update) | async-done | bytes 786448 | tf_op jit(solution)/shard_map/reduce_scatter | solution.py:54
  86.0 42.4 %all-gather.10.cloned.1.call-done = bf16[4096,768]{1,0:T(8,128)(2,1)} async-done(((bf16[1024,768]{1,0:T(8,128)(2,1)}), bf16[4096,768]{1,0:T(8,128)(2,1)}) %all-gather.10.cloned.1.call-update) | async-done | bytes 6291472 | tf_op jit(solution)/shard_map/all_gather | solution.py:172
  128.4 5.1 convolution_convert_fusion
  135.4 2.2 convolution_convert_fusion.1
  139.4 10.8 %all-gather.12.cloned.1.call-done = bf16[1024,768]{1,0:T(8,128)(2,1)} async-done(((bf16[256,768]{1,0:T(8,128)(2,1)}), bf16[1024,768]{1,0:T(8,128)(2,1)}) %all-gather.12.cloned.1.call-update) | async-done | bytes 1572880 | tf_op jit(solution)/shard_map/all_gather | solution.py:32
  150.2 2.2 fusion.27
  157.2 2.2 fusion.34
  160.5 2.3 fusion.71
  163.4 37.5 %reduce-scatter.10.cloned.1.call-done = f32[256,768]{1,0:T(8,128)} async-done(((f32[1024,768]{1,0:T(8,128)}), f32[256,768]{1,0:T(8,128)}) %reduce-scatter.10.cloned.1.call-update) | async-done | bytes 786448 | tf_op jit(solution)/shard_map/reduce_scatter | solution.py:54
  204.6 17.4 %all-gather.16.cloned.1.call-done = bf16[1024,768]{1,0:T(8,128)(2,1)} async-done(((bf16[256,768]{1,0:T(8,128)(2,1)}), bf16[1024,768]{1,0:T(8,128)(2,1)}) %all-gather.16.cloned.1.call-update) | async-done | bytes 1572880 | tf_op jit(solution)/shard_map/all_gather | solution.py:36
  222.0 4.8 fusion.114
  226.8 17.0 %all-gather.14.cloned.1.call-done = bf16[1024,768]{1,0:T(8,128)(2,1)} async-done(((bf16[256,768]{1,0:T(8,128)(2,1)}), bf16[1024,768]{1,0:T(8,128)(2,1)}) %all-gather.14.cloned.1.call-update) | async-done | bytes 1572880 | tf_op jit(solution)/shard_map/all_gather | solution.py:32
  243.8 6.9 fusion.4
  251.9 3.1 fusion.115
  256.2 5.5 fusion.110
  261.8 31.3 %reduce-scatter.14.cloned.1.call-done = f32[256,768]{1,0:T(8,128)} async-done(((f32[1024,768]{1,0:T(8,128)}), f32[256,768]{1,0:T(8,128)}) %reduce-scatter.14.cloned.1.call-update) | async-done | bytes 786448 | tf_op jit(solution)/shard_map/reduce_scatter | solution.py:66
  295.6 38.2 %reduce-scatter.12.cloned.1.call-done = f32[256,768]{1,0:T(8,128)} async-done(((f32[1024,768]{1,0:T(8,128)}), f32[256,768]{1,0:T(8,128)}) %reduce-scatter.12.cloned.1.call-update) | async-done | bytes 786448 | tf_op jit(solution)/shard_map/reduce_scatter | solution.py:54
  333.8 2.8 fusion.112
  336.7 19.8 %all-gather.18.cloned.1.call-done = bf16[1024,768]{1,0:T(8,128)(2,1)} async-done(((bf16[256,768]{1,0:T(8,128)(2,1)}), bf16[1024,768]{1,0:T(8,128)(2,1)}) %all-gather.18.cloned.1.call-update) | async-done | bytes 1572880 | tf_op jit(solution)/shard_map/all_gather | solution.py:36
  356.5 2.2 fusion.28
  358.8 5.7 multiply_reduce_fusion
  368.2 2.3 fusion.67
  370.5 38.1 %reduce-scatter.16.cloned.1.call-done = f32[256,768]{1,0:T(8,128)} async-done(((f32[1024,768]{1,0:T(8,128)}), f32[256,768]{1,0:T(8,128)}) %reduce-scatter.16.cloned.1.call-update) | async-done | bytes 786448 | tf_op jit(solution)/shard_map/reduce_scatter | solution.py:66
  410.5 2.6 fusion.111
  413.7 4.0 fusion.9
  425.0 4.6 add_convert_fusion
  429.7 3.3 all-gather.20.cloned.1.call-done
  433.0 2.1 fusion.29
  435.2 2.2 fusion.33
  442.5 2.7 add_add_fusion
  445.5 5.3 fusion.117
  450.8 5.3 fusion.109
  459.5 2.2 convolution_bitcast_fusion
  461.7 2.2 convolution_bitcast_fusion.1
  471.4 22.7 %reduce-scatter.20.cloned.1.call-done = bf16[1024,768]{1,0:T(8,128)(2,1)} async-done(((bf16[4096,768]{1,0:T(8,128)(2,1)}), bf16[1024,768]{1,0:T(8,128)(2,1)}) %reduce-scatter.20.cloned.1.call-update) | async-done | bytes 1572880 | tf_op jit(solution)/shard_map/reduce_scatter | solution.py:221
  494.1 3.3 convert_element_type.162
  497.4 37.1 %reduce-scatter.18.cloned.1.call-done = f32[256,768]{1,0:T(8,128)} async-done(((f32[1024,768]{1,0:T(8,128)}), f32[256,768]{1,0:T(8,128)}) %reduce-scatter.18.cloned.1.call-update) | async-done | bytes 786448 | tf_op jit(solution)/shard_map/reduce_scatter | solution.py:66
  535.9 10.1 %all-reduce.2 = (f32[768]{0:T(1024)S(1)}, f32[768]{0:T(1024)S(1)}, f32[768]{0:T(1024)S(1)}) all-reduce(f32[768]{0:T(1024)S(1)} %get-tuple-element.21, f32[768]{0:T(1024)S(1)} %copy-done.77, f32[768]{0:T(1024)S(1)} %copy-done.76), channel_id=1, replica_groups=mesh['dp'=8,'mp'=4] {'mp'}, use_global_device_ids=true, to_apply=%region_21.22 | all-reduce | flops 2304 | bytes 18432 | tf_op jit(solution)/shard_map/psum | solution.py:247
  546.0 39.8 %all-reduce = (f32[768]{0:T(1024)}, f32[32,3]{0,1:T(4,128)}, f32[768]{0:T(1024)}, f32[768]{0:T(1024)}) all-reduce(f32[768]{0:T(1024)S(1)} %get-tuple-element.37, f32[32,3]{0,1:T(4,128)S(1)} %convolution_bitcast_fusion.3, f32[768]{0:T(1024)S(1)} %get-tuple-element.38, ...), channel_id=1, replica_groups=mesh['dp'=8,'mp'=4] {'dp'}, use_global_device_ids=true, to_apply=%region_22.23 | all-reduce | flops 2400 | bytes 19200 | tf_op jit(solution)/shard_map/psum | solution.py:250
  585.8 2.3 fusion.46
  588.1 260.6 %all-reduce.5.cloned.1.call-done = (f32[768,192]{0,1:T(8,128)}, f32[768,192]{0,1:T(8,128)}, f32[768,192]{0,1:T(8,128)}, f32[192,768]{1,0:T(8,128)}, f32[768,192]...) async-done(((f32[768,192]{0,1:T(8,128)}, f32[768,192]{0,1:T(8,128)}, ...) | async-done | bytes 9437200 | tf_op jit(solution)/shard_map/psum | solution.py:250
  848.7 2.0 copy.290
  850.7 2.0 copy.291
  (294 shorter events, 75.1 us)
Async XLA Ops:
  7.2 236.6 %copy-start = (bf16[768,768]{1,0:T(8,128)(2,1)S(1)}, bf16[768,768]{1,0:T(8,128)(2,1)}, u32[]{:S(2)}) copy-start(bf16[768,768]{1,0:T(8,128)(2,1)} %param.37) | copy-start | bytes 3538948
  7.2 12.9 %copy-start.83 = (f32[32,3]{0,1:T(4,128)S(1)}, f32[32,3]{0,1:T(4,128)}, u32[]{:S(2)}) copy-start(f32[32,3]{0,1:T(4,128)} %param.30) | copy-start | bytes 1156
  7.2 13.6 %copy-start.87 = (s32[8]{0:T(128)S(1)}, s32[8]{0:T(128)}, u32[]{:S(2)}) copy-start(s32[8]{0:T(128)} %param.22) | copy-start | bytes 100
  7.2 26.3 %all-gather.8.cloned.1.call-start = ((), (), s32[]{:S(2)}) async-start(), calls=%async_computation.7 | async-start | bytes 1966080 | tf_op jit(solution)/shard_map/all_gather | solution.py:32
  8.5 25.0 %copy-start.48 = (bf16[768,192]{0,1:T(8,128)(2,1)S(1)}, bf16[768,192]{0,1:T(8,128)(2,1)}, u32[]{:S(2)}) copy-start(bf16[768,192]{0,1:T(8,128)(2,1)} %param.27) | copy-start | bytes 884740
  9.1 7.9 copy-start.74
  11.0 69.3 %reduce-scatter.8.cloned.1.call-start = ((), (), s32[]{:S(2)}) async-start(), calls=%async_computation.8 | async-start | bytes 3932160 | tf_op jit(solution)/shard_map/reduce_scatter | solution.py:54
  17.0 4.8 copy-start.66
  20.1 15.8 %copy-start.46 = (bf16[768,192]{0,1:T(8,128)(2,1)S(1)}, bf16[768,192]{0,1:T(8,128)(2,1)}, u32[]{:S(2)}) copy-start(bf16[768,192]{0,1:T(8,128)(2,1)} %param.26) | copy-start | bytes 884740
  42.3 86.2 %all-gather.10.cloned.1.call-start = ((), (), s32[]{:S(2)}) async-start(), calls=%async_computation.9 | async-start | bytes 7864320 | tf_op jit(solution)/shard_map/all_gather | solution.py:172
  43.0 107.2 %all-gather.12.cloned.1.call-start = ((), (), s32[]{:S(2)}) async-start(), calls=%async_computation.10 | async-start | bytes 1966080 | tf_op jit(solution)/shard_map/all_gather | solution.py:32
  84.5 116.4 %reduce-scatter.10.cloned.1.call-start = ((), (), s32[]{:S(2)}) async-start(), calls=%async_computation.11 | async-start | bytes 3932160 | tf_op jit(solution)/shard_map/reduce_scatter | solution.py:54
  128.4 6.9 copy-start.84
  162.8 59.2 %all-gather.16.cloned.1.call-start = ((), (), s32[]{:S(2)}) async-start(), calls=%async_computation.14 | async-start | bytes 1966080 | tf_op jit(solution)/shard_map/all_gather | solution.py:36
  163.4 80.5 %all-gather.14.cloned.1.call-start = ((), (), s32[]{:S(2)}) async-start(), calls=%async_computation.12 | async-start | bytes 1966080 | tf_op jit(solution)/shard_map/all_gather | solution.py:32
  204.3 88.8 %reduce-scatter.14.cloned.1.call-start = ((), (), s32[]{:S(2)}) async-start(), calls=%async_computation.15 | async-start | bytes 3932160 | tf_op jit(solution)/shard_map/reduce_scatter | solution.py:66
  255.0 78.8 %reduce-scatter.12.cloned.1.call-start = ((), (), s32[]{:S(2)}) async-start(), calls=%async_computation.13 | async-start | bytes 3932160 | tf_op jit(solution)/shard_map/reduce_scatter | solution.py:54
  261.7 31.4 %copy-start.11 = (f32[256,768]{1,0:T(8,128)S(1)}, f32[256,768]{1,0:T(8,128)}, u32[]{:S(2)}) copy-start(f32[256,768]{1,0:T(8,128)} %copy-done.10) | copy-start | bytes 2359300
  261.7 72.0 %copy-start.39 = (bf16[256,768]{1,0:T(8,128)(2,1)S(1)}, bf16[256,768]{1,0:T(8,128)(2,1)}, u32[]{:S(2)}) copy-start(bf16[256,768]{1,0:T(8,128)(2,1)} %param.39) | copy-start | bytes 1179652
  261.8 94.7 %all-gather.18.cloned.1.call-start = ((), (), s32[]{:S(2)}) async-start(), calls=%async_computation.16 | async-start | bytes 1966080 | tf_op jit(solution)/shard_map/all_gather | solution.py:36
  336.6 22.2 %copy-start.63 = (f32[8,3,128]{2,1,0:T(4,128)S(1)}, f32[8,3,128]{2,1,0:T(4,128)}, u32[]{:S(2)}) copy-start(f32[8,3,128]{2,1,0:T(4,128)} %copy-done.62) | copy-start | bytes 36868
  336.6 22.2 %copy-start.69 = (pred[8,512]{1,0:T(8,128)(4,1)S(1)}, pred[8,512]{1,0:T(8,128)(4,1)}, u32[]{:S(2)}) copy-start(pred[8,512]{1,0:T(8,128)(4,1)} %iota_compare_fusion.3) | copy-start | bytes 12292
  336.6 71.9 %reduce-scatter.16.cloned.1.call-start = ((), (), s32[]{:S(2)}) async-start(), calls=%async_computation.17 | async-start | bytes 3932160 | tf_op jit(solution)/shard_map/reduce_scatter | solution.py:66
  358.8 5.8 slice-start
  358.8 5.7 slice-start.1
  370.4 38.1 %copy-start.73 = (f32[768]{0:T(1024)S(1)}, f32[768]{0:T(1024)}, u32[]{:S(2)}) copy-start(f32[768]{0:T(1024)} %param.31) | copy-start | bytes 9220
  370.4 38.1 %copy-start.79 = (f32[256]{0:T(256)S(1)}, f32[256]{0:T(256)}, u32[]{:S(2)}) copy-start(f32[256]{0:T(256)} %copy-done.78) | copy-start | bytes 3076
  370.4 40.1 %copy-start.82 = (f32[256]{0:T(256)S(1)}, f32[256]{0:T(256)}, u32[]{:S(2)}) copy-start(f32[256]{0:T(256)} %get-tuple-element.53) | copy-start | bytes 3076
  370.5 62.5 %all-gather.20.cloned.1.call-start = ((), (), s32[]{:S(2)}) async-start(), calls=%async_computation.18 | async-start | bytes 1966080 | tf_op jit(solution)/shard_map/all_gather | solution.py:36
  413.2 80.9 %reduce-scatter.20.cloned.1.call-start = ((), (), s32[]{:S(2)}) async-start(), calls=%async_computation.20 | async-start | bytes 7864320 | tf_op jit(solution)/shard_map/reduce_scatter | solution.py:221
  429.6 104.8 %reduce-scatter.18.cloned.1.call-start = ((), (), s32[]{:S(2)}) async-start(), calls=%async_computation.19 | async-start | bytes 3932160 | tf_op jit(solution)/shard_map/reduce_scatter | solution.py:66
  445.3 403.4 %all-reduce.5.cloned.1.call-start = ((), (), s32[]{:S(2)}) async-start(), calls=%async_computation.21 | async-start | bytes 18874368 | tf_op jit(solution)/shard_map/psum | solution.py:250
  445.5 5.3 copy-start.85
  445.5 14.0 %slice-start.2 = ((s8[6291456]{0:T(1024)(128)(4,1)}), s8[4194304]{0:T(1024)(128)(4,1)S(1)}, s32[]{:S(2)}) async-start(s8[6291456]{0:T(1024)(128)(4,1)} %bitcast.226), calls=%async_computation.24 | async-start | bytes 8388608
  450.8 5.3 copy-start.16
  450.8 5.3 copy-start.27
  450.8 6.6 copy-start.29
  450.8 8.6 slice-start.3
  471.4 63.1 %copy-start.12 = (bf16[256,768]{1,0:T(8,128)(2,1)S(1)}, bf16[256,768]{1,0:T(8,128)(2,1)}, u32[]{:S(2)}) copy-start(bf16[256,768]{1,0:T(8,128)(2,1)} %param.20) | copy-start | bytes 1179652
  471.4 63.1 %copy-start.72 = (f32[768]{0:T(1024)S(1)}, f32[768]{0:T(1024)}, u32[]{:S(2)}) copy-start(f32[768]{0:T(1024)} %param.25) | copy-start | bytes 9220
  471.4 63.1 %copy-start.75 = (f32[256]{0:T(256)S(1)}, f32[256]{0:T(256)}, u32[]{:S(2)}) copy-start(f32[256]{0:T(256)} %copy-done.74) | copy-start | bytes 3076
  471.4 64.5 %copy-start.76 = (f32[768]{0:T(1024)S(1)}, f32[768]{0:T(1024)}, u32[]{:S(2)}) copy-start(f32[768]{0:T(1024)} %get-tuple-element.17) | copy-start | bytes 9220
  471.4 64.5 %copy-start.77 = (f32[768]{0:T(1024)S(1)}, f32[768]{0:T(1024)}, u32[]{:S(2)}) copy-start(f32[768]{0:T(1024)} %get-tuple-element.19) | copy-start | bytes 9220
  471.4 114.4 %copy-start.36 = (f32[256,768]{1,0:T(8,128)S(1)}, f32[256,768]{1,0:T(8,128)}, u32[]{:S(2)}) copy-start(f32[256,768]{1,0:T(8,128)} %get-tuple-element.41) | copy-start | bytes 2359300
  471.4 114.4 %copy-start.81 = (f32[256]{0:T(256)S(1)}, f32[256]{0:T(256)}, u32[]{:S(2)}) copy-start(f32[256]{0:T(256)} %get-tuple-element.51) | copy-start | bytes 3076
  848.6 4.9 copy-start.54
  848.6 5.7 copy-start.53
  850.7 4.4 copy-start.52
  (60 other events, 120.0 us)
Sparse Core Ops, SparseCore 0:
  11.2 22.3 all-gather.7
  42.4 37.9 reduce-scatter.7
  82.0 46.3 all-gather.9
  130.5 19.6 all-gather.11
  162.9 37.9 reduce-scatter.9
  202.3 19.6 all-gather.15
  224.1 19.6 all-gather.13
  255.1 37.9 reduce-scatter.13
  295.8 37.9 reduce-scatter.11
  336.8 19.6 all-gather.17
  370.6 37.9 reduce-scatter.15
  413.3 19.6 all-gather.19
  435.7 58.3 reduce-scatter.19
  496.5 37.9 reduce-scatter.17
  543.3 305.2 all-reduce.4
where the time goes:
time: 875 us; the launch traced here: 868 us
  waiting for transfers between devices  627 us (72%)
  matrix products  99.8 us (11%)
  blocking collectives  49.9 us (6%)
  other arithmetic  40.4 us (5%)
  local copies, waits for them, and re-layouts  34.8 us (4%)
  between operations  15.2 us (2%)
    psum x1, waiting for transfers between devices, body(): lax.psum((gain_one, self_query_part, self_key_part, self_value_part, self...  261 us
    reduce_scatter x3, waiting for transfers between devices, branch_sum(): lax.psum_scatter(jnp.dot(mixed, weight, preferred_element_type=jnp.float3...  113 us
    reduce_scatter x3, waiting for transfers between devices, input_sum(): return lax.psum_scatter(summed, 'mp', scatter_dimension=0, tiled=True)  106 us
    all_gather x1, waiting for transfers between devices, body(): memory_all = lax.all_gather(memory, 'mp', axis=0, tiled=True)  42.4 us
    all_gather x3, waiting for transfers between devices, gather_upstream(): return lax.all_gather(values, 'mp', axis=0, tiled=True)  40.5 us
    psum x1, blocking collectives, body(): lax.psum((gain_one, self_query_part, self_key_part, self_value_part, self...  39.8 us
    all_gather x3, waiting for transfers between devices, gather_normed(): return lax.all_gather(values, 'mp', axis=0, tiled=True)  39.6 us
    unnamed x206, local copies, waits for them, and re-layouts  28.8 us
  transfers between devices with their start and end apart: 15, of which 15 were waited for; matrix products, arithmetic and copies ran while one was open for 11% of the time, Pallas kernels for 0%

commit v1 on v0

--- a/solution.py
+++ b/solution.py
@@ -2,6 +2,7 @@
 import jax.numpy as jnp
 from jax import lax
 from jax.sharding import PartitionSpec as P
+from jax.lax import axis_index, axis_size, ppermute
 
 HEAD_DIM = 64
 BUCKETS = 32
@@ -14,6 +15,34 @@
 cubic_term = 0.044715
 
 
+def state_quotas(here_x, where_dim):
+    fresh = list(here_x.shape[1:])
+    fresh[where_dim] *= here_x.shape[0]
+    block_last = jnp.moveaxis(here_x, 0, where_dim).reshape(fresh)
+    return block_last
+
+
+def sector_start(load, mesh_ax, ndim_at):
+    extent = axis_size(mesh_ax)
+    by_rank = list(map(lambda kk: (kk, (kk + 1) % extent), range(extent)))
+    heap = [(jj, u) for u, jj in by_rank]
+    arr_next, block_next = ([], [])
+    for w in range(extent - 1):
+        if w % 2 == 0:
+            arr_next.append(
+                ppermute(arr_next[-1] if arr_next else load, perm=by_rank, axis_name=mesh_ax)
+            )
+        else:
+            block_next.append(
+                ppermute(block_next[-1] if block_next else load, axis_name=mesh_ax, perm=heap)
+            )
+    field_out = jnp.stack([*arr_next[::-1], load, *block_next], 0)
+    n_now = axis_index(mesh_ax) - len(arr_next)
+    field_out = field_out[(jnp.arange(extent) - n_now) % extent]
+    x_next = state_quotas(field_out, ndim_at)
+    return x_next
+
+
 def gelu_tanh(value):
     return 0.5 * value * (1.0 + jnp.tanh(tanh_scale * (value + cubic_term * value * value * value)))
 
@@ -33,7 +62,7 @@
 
 
 def gather_upstream(values):
-    return lax.all_gather(values, "mp", axis=0, tiled=True)
+    return sector_start(values, "mp", ndim_at=0)
 
 
 def project(rows, weight):

time: 875 us -> 845 us (0.966)
  waiting for transfers between devices: 627 us -> 583 us
  local copies, waits for them, and re-layouts: 34.8 us -> 45.8 us
    ppermute x0 -> x9, waiting for transfers between devices: none -> 54.2 us  [the longest x6 53.7 us: sector_start(): ppermute(arr_next[-1] if arr_next else load, perm=by_rank, axis_name=mesh...]
    all_gather x3 -> x0, waiting for transfers between devices: 40.5 us -> none  [gather_upstream(): return lax.all_gather(values, 'mp', axis=0, tiled=True)]
    reduce_scatter x1, waiting for transfers between devices: 22.7 us -> 0.02 us  [body(): lax.psum_scatter((back_project(cross_k_grad, cross_key) + back_project(cr...]
    reduce_scatter x3, waiting for transfers between devices: 106 us -> 86.9 us  [input_sum(): return lax.psum_scatter(summed, 'mp', scatter_dimension=0, tiled=True)]
    all_gather x3, waiting for transfers between devices: 39.6 us -> 23.2 us  [gather_normed(): return lax.all_gather(values, 'mp', axis=0, tiled=True)]
    gather x0 -> x3, local copies, waits for them, and re-layouts: none -> 10.5 us  [sector_start(): field_out = field_out[(jnp.arange(extent) - n_now) % extent]]
    unnamed x206 -> x222, local copies, waits for them, and re-layouts: 28.8 us -> 29.4 us
  transfers between devices with their start and end apart: 15 -> 21, of which waited for: 15 -> 17; matrix products, arithmetic and copies ran while one was open for 11% -> 12% of each run, Pallas kernels for 0% -> 0%
where the time goes in v1:
time: 845 us; the launch traced here: 838 us
  waiting for transfers between devices  583 us (69%)
  matrix products  93 us (11%)
  blocking collectives  49.9 us (6%)
  local copies, waits for them, and re-layouts  45.8 us (5%)
  other arithmetic  43.9 us (5%)
  between operations  15.5 us (2%)
    psum x1, waiting for transfers between devices, body(): lax.psum((gain_one, self_query_part, self_key_part, self_value_part, self...  262 us
    reduce_scatter x3, waiting for transfers between devices, branch_sum(): lax.psum_scatter(jnp.dot(mixed, weight, preferred_element_type=jnp.float3...  114 us
    reduce_scatter x3, waiting for transfers between devices, input_sum(): return lax.psum_scatter(summed, 'mp', scatter_dimension=0, tiled=True)  86.9 us
    ppermute x6, waiting for transfers between devices, sector_start(): ppermute(arr_next[-1] if arr_next else load, perm=by_rank, axis_name=mesh...  53.7 us
    all_gather x1, waiting for transfers between devices, body(): memory_all = lax.all_gather(memory, 'mp', axis=0, tiled=True)  42.4 us
    psum x1, blocking collectives, body(): lax.psum((gain_one, self_query_part, self_key_part, self_value_part, self...  39.8 us
    unnamed x222, local copies, waits for them, and re-layouts  29.4 us
    dot_general x10, matrix products, back_project(): lax.dot_general(grad_rows, weight, (((1,), (1,)), ((), ())), preferred_el...  23.8 us
  transfers between devices with their start and end apart: 21, of which 17 were waited for; matrix products, arithmetic and copies ran while one was open for 12% of the time, Pallas kernels for 0%

profile of v1, /device:TPU:0, one launch (start us, length us, event | category | flops | bytes accessed | tf_op | source)
XLA Modules:
  0.0 837.6 jit_solution(15409539745249560672)
XLA Ops:
  11.1 5.1 select_reduce_fusion
  17.0 2.4 copy.123
  21.2 12.4 %all-gather.5.cloned.1.call-done = bf16[1024,768]{1,0:T(8,128)(2,1)} async-done(((bf16[256,768]{1,0:T(8,128)(2,1)}), bf16[1024,768]{1,0:T(8,128)(2,1)}) %all-gather.5.cloned.1.call-update) | async-done | bytes 1572880 | tf_op jit(solution)/shard_map/all_gather | solution.py:61
  33.6 2.2 fusion.26
  40.6 2.3 fusion.75
  43.7 37.3 %reduce-scatter.8.cloned.1.call-done = f32[256,768]{1,0:T(8,128)} async-done(((f32[1024,768]{1,0:T(8,128)}), f32[256,768]{1,0:T(8,128)}) %reduce-scatter.8.cloned.1.call-update) | async-done | bytes 786448 | tf_op jit(solution)/shard_map/reduce_scatter | solution.py:83
  86.7 42.4 %all-gather.7.cloned.1.call-done = bf16[4096,768]{1,0:T(8,128)(2,1)} async-done(((bf16[1024,768]{1,0:T(8,128)(2,1)}), bf16[4096,768]{1,0:T(8,128)(2,1)}) %all-gather.7.cloned.1.call-update) | async-done | bytes 6291472 | tf_op jit(solution)/shard_map/all_gather | solution.py:201
  129.1 5.1 convolution_convert_fusion
  136.1 2.2 convolution_convert_fusion.1
  140.0 10.8 %all-gather.9.cloned.1.call-done = bf16[1024,768]{1,0:T(8,128)(2,1)} async-done(((bf16[256,768]{1,0:T(8,128)(2,1)}), bf16[1024,768]{1,0:T(8,128)(2,1)}) %all-gather.9.cloned.1.call-update) | async-done | bytes 1572880 | tf_op jit(solution)/shard_map/all_gather | solution.py:61
  150.9 2.2 fusion.27
  157.9 2.2 fusion.34
  161.1 2.3 fusion.71
  163.5 38.1 %reduce-scatter.10.cloned.1.call-done = f32[256,768]{1,0:T(8,128)} async-done(((f32[1024,768]{1,0:T(8,128)}), f32[256,768]{1,0:T(8,128)}) %reduce-scatter.10.cloned.1.call-update) | async-done | bytes 786448 | tf_op jit(solution)/shard_map/reduce_scatter | solution.py:83
  206.8 10.5 %collective-permute-done = bf16[256,768]{1,0:T(8,128)(2,1)} collective-permute-done((bf16[256,768]{1,0:T(8,128)(2,1)}, bf16[256,768]{1,0:T(8,128)(2,1)}, u32[]{:S(2)}, u32[]{:S(2)}) %collective-permute-start) | collective-permute-done | bytes 393248 | tf_op jit(solution)/shard_map/ppermute | solution.py:33
  218.8 10.6 %collective-permute-done.1 = bf16[256,768]{1,0:T(8,128)(2,1)} collective-permute-done((bf16[256,768]{1,0:T(8,128)(2,1)}, bf16[256,768]{1,0:T(8,128)(2,1)}, u32[]{:S(2)}, u32[]{:S(2)}) %collective-permute-start.1) | collective-permute-done | bytes 393248 | tf_op jit(solution)/shard_map/ppermute | solution.py:33
  229.4 2.7 pad_maximum_fusion
  232.1 3.3 gather_fusion
  235.4 2.9 fusion.116
  238.4 4.0 fusion.4
  243.7 3.1 fusion.117
  248.1 5.5 fusion.112
  253.7 31.3 %reduce-scatter.14.cloned.1.call-done = f32[256,768]{1,0:T(8,128)} async-done(((f32[1024,768]{1,0:T(8,128)}), f32[256,768]{1,0:T(8,128)}) %reduce-scatter.14.cloned.1.call-update) | async-done | bytes 786448 | tf_op jit(solution)/shard_map/reduce_scatter | solution.py:95
  287.5 38.2 %reduce-scatter.12.cloned.1.call-done = f32[256,768]{1,0:T(8,128)} async-done(((f32[1024,768]{1,0:T(8,128)}), f32[256,768]{1,0:T(8,128)}) %reduce-scatter.12.cloned.1.call-update) | async-done | bytes 786448 | tf_op jit(solution)/shard_map/reduce_scatter | solution.py:83
  325.7 2.7 fusion.114
  330.2 9.1 %collective-permute-done.3 = bf16[256,768]{1,0:T(8,128)(2,1)S(1)} collective-permute-done((bf16[256,768]{1,0:T(8,128)(2,1)S(1)}, bf16[256,768]{1,0:T(8,128)(2,1)S(1)}, u32[]{:S(2)}, u32[]{:S(2)}) %collective-permute-start.3) | collective-permute-done | bytes 393248 | tf_op jit(solution)/shard_map/ppermute | solution.py:33
  339.3 7.2 collective-permute-done.4
  347.8 3.4 gather_fusion.1
  351.2 2.2 fusion.28
  353.5 5.8 multiply_reduce_fusion
  362.9 2.3 fusion.67
  366.0 4.0 fusion.9
  377.2 4.6 add_convert_fusion
  381.8 21.3 %reduce-scatter.16.cloned.1.call-done = f32[256,768]{1,0:T(8,128)} async-done(((f32[1024,768]{1,0:T(8,128)}), f32[256,768]{1,0:T(8,128)}) %reduce-scatter.16.cloned.1.call-update) | async-done | bytes 786448 | tf_op jit(solution)/shard_map/reduce_scatter | solution.py:95
  408.7 9.1 %collective-permute-done.6 = bf16[256,768]{1,0:T(8,128)(2,1)S(1)} collective-permute-done((bf16[256,768]{1,0:T(8,128)(2,1)S(1)}, bf16[256,768]{1,0:T(8,128)(2,1)S(1)}, u32[]{:S(2)}, u32[]{:S(2)}) %collective-permute-start.6) | collective-permute-done | bytes 393248 | tf_op jit(solution)/shard_map/ppermute | solution.py:33
  417.9 7.2 collective-permute-done.7
  426.4 3.8 gather_fusion.2
  430.2 2.2 fusion.29
  439.0 2.3 add_add_fusion
  441.6 4.9 fusion.119
  446.5 5.4 fusion.111
  455.0 2.2 convolution_bitcast_fusion
  457.2 2.2 convolution_bitcast_fusion.1
  467.0 3.4 convert_element_type.162
  470.4 34.3 %reduce-scatter.18.cloned.1.call-done = f32[256,768]{1,0:T(8,128)} async-done(((f32[1024,768]{1,0:T(8,128)}), f32[256,768]{1,0:T(8,128)}) %reduce-scatter.18.cloned.1.call-update) | async-done | bytes 786448 | tf_op jit(solution)/shard_map/reduce_scatter | solution.py:95
  506.1 10.1 %all-reduce.2 = (f32[768]{0:T(1024)S(1)}, f32[768]{0:T(1024)S(1)}, f32[768]{0:T(1024)S(1)}) all-reduce(f32[768]{0:T(1024)S(1)} %get-tuple-element.21, f32[768]{0:T(1024)S(1)} %copy-done.84, f32[768]{0:T(1024)S(1)} %copy-done.83), channel_id=1, replica_groups=mesh['dp'=8,'mp'=4] {'mp'}, use_global_device_ids=true, to_apply=%region_21.22 | all-reduce | flops 2304 | bytes 18432 | tf_op jit(solution)/shard_map/psum | solution.py:276
  516.3 39.8 %all-reduce = (f32[768]{0:T(1024)}, f32[32,3]{0,1:T(4,128)}, f32[768]{0:T(1024)}, f32[768]{0:T(1024)}) all-reduce(f32[768]{0:T(1024)S(1)} %get-tuple-element.37, f32[32,3]{0,1:T(4,128)S(1)} %convolution_bitcast_fusion.3, f32[768]{0:T(1024)S(1)} %get-tuple-element.38, ...), channel_id=1, replica_groups=mesh['dp'=8,'mp'=4] {'dp'}, use_global_device_ids=true, to_apply=%region_22.23 | all-reduce | flops 2400 | bytes 19200 | tf_op jit(solution)/shard_map/psum | solution.py:279
  557.2 261.7 %all-reduce.5.cloned.1.call-done = (f32[768,192]{0,1:T(8,128)}, f32[768,192]{0,1:T(8,128)}, f32[768,192]{0,1:T(8,128)}, f32[192,768]{1,0:T(8,128)}, f32[768,192]...) async-done(((f32[768,192]{0,1:T(8,128)}, f32[768,192]{0,1:T(8,128)}, ...) | async-done | bytes 9437200 | tf_op jit(solution)/shard_map/psum | solution.py:279
  (327 shorter events, 91.8 us)
Async XLA Ops:
  7.2 228.2 %copy-start = (bf16[768,768]{1,0:T(8,128)(2,1)S(1)}, bf16[768,768]{1,0:T(8,128)(2,1)}, u32[]{:S(2)}) copy-start(bf16[768,768]{1,0:T(8,128)(2,1)} %param.37) | copy-start | bytes 3538948
  7.2 26.3 %all-gather.5.cloned.1.call-start = ((), (), s32[]{:S(2)}) async-start(), calls=%async_computation.7 | async-start | bytes 1966080 | tf_op jit(solution)/shard_map/all_gather | solution.py:61
  9.1 10.3 %copy-start.89 = (f32[32,3]{0,1:T(4,128)S(1)}, f32[32,3]{0,1:T(4,128)}, u32[]{:S(2)}) copy-start(f32[32,3]{0,1:T(4,128)} %param.30) | copy-start | bytes 1156
  11.0 70.0 %reduce-scatter.8.cloned.1.call-start = ((), (), s32[]{:S(2)}) async-start(), calls=%async_computation.8 | async-start | bytes 3932160 | tf_op jit(solution)/shard_map/reduce_scatter | solution.py:83
  11.1 9.1 %copy-start.94 = (s32[8]{0:T(128)S(1)}, s32[8]{0:T(128)}, u32[]{:S(2)}) copy-start(s32[8]{0:T(128)} %param.22) | copy-start | bytes 100
  16.3 17.3 %copy-start.54 = (bf16[768,192]{0,1:T(8,128)(2,1)S(1)}, bf16[768,192]{0,1:T(8,128)(2,1)}, u32[]{:S(2)}) copy-start(bf16[768,192]{0,1:T(8,128)(2,1)} %param.27) | copy-start | bytes 884740
  16.4 4.7 copy-start.73
  20.3 15.5 %copy-start.52 = (bf16[768,192]{0,1:T(8,128)(2,1)S(1)}, bf16[768,192]{0,1:T(8,128)(2,1)}, u32[]{:S(2)}) copy-start(bf16[768,192]{0,1:T(8,128)(2,1)} %param.26) | copy-start | bytes 884740
  42.9 86.2 %all-gather.7.cloned.1.call-start = ((), (), s32[]{:S(2)}) async-start(), calls=%async_computation.9 | async-start | bytes 7864320 | tf_op jit(solution)/shard_map/all_gather | solution.py:201
  43.7 107.2 %all-gather.9.cloned.1.call-start = ((), (), s32[]{:S(2)}) async-start(), calls=%async_computation.10 | async-start | bytes 1966080 | tf_op jit(solution)/shard_map/all_gather | solution.py:61
  85.2 116.3 %reduce-scatter.10.cloned.1.call-start = ((), (), s32[]{:S(2)}) async-start(), calls=%async_computation.11 | async-start | bytes 3932160 | tf_op jit(solution)/shard_map/reduce_scatter | solution.py:83
  129.1 6.9 copy-start.91
  163.4 72.0 %all-gather.11.cloned.1.call-start = ((), (), s32[]{:S(2)}) async-start(), calls=%async_computation.12 | async-start | bytes 1966080 | tf_op jit(solution)/shard_map/all_gather | solution.py:61
  204.9 80.1 %reduce-scatter.14.cloned.1.call-start = ((), (), s32[]{:S(2)}) async-start(), calls=%async_computation.14 | async-start | bytes 3932160 | tf_op jit(solution)/shard_map/reduce_scatter | solution.py:95
  205.0 12.3 %collective-permute-start = (bf16[256,768]{1,0:T(8,128)(2,1)}, bf16[256,768]{1,0:T(8,128)(2,1)}, u32[]{:S(2)}, u32[]{:S(2)}) collective-permute-start(bf16[256,768]{1,0:T(8,128)(2,1)} %param.39), channel_id=1, source_target_pairs={{0,1},{1,2},{2,3},{3,0},{4,5},{5,6},{6,7},{7,4},{8,9},{9,10},{10,1... | collective-permute-start | bytes 1179656 | tf_op jit(solution)/shard_map/ppermute | solution.py:33
  205.1 13.7 %collective-permute-start.2 = (bf16[256,768]{1,0:T(8,128)(2,1)}, bf16[256,768]{1,0:T(8,128)(2,1)}, u32[]{:S(2)}, u32[]{:S(2)}) collective-permute-start(bf16[256,768]{1,0:T(8,128)(2,1)} %param.39), channel_id=1, source_target_pairs={{1,0},{2,1},{3,2},{0,3},{5,4},{6,5},{7,6},{4,7},{9,8},{10,9},{11,1... | collective-permute-start | bytes 1179656 | tf_op jit(solution)/shard_map/ppermute | solution.py:37
  217.3 12.1 %collective-permute-start.1 = (bf16[256,768]{1,0:T(8,128)(2,1)}, bf16[256,768]{1,0:T(8,128)(2,1)}, u32[]{:S(2)}, u32[]{:S(2)}) collective-permute-start(bf16[256,768]{1,0:T(8,128)(2,1)} %collective-permute-done), channel_id=1, source_target_pairs={{0,1},{1,2},{2,3},{3,0},{4,5},{5,6},{6,7},{7,4},{8,9},{9,10},{10,1... | collective-permute-start | bytes 1179656 | tf_op jit(solution)/shard_map/ppermute | solution.py:33
  246.8 78.8 %reduce-scatter.12.cloned.1.call-start = ((), (), s32[]{:S(2)}) async-start(), calls=%async_computation.13 | async-start | bytes 3932160 | tf_op jit(solution)/shard_map/reduce_scatter | solution.py:83
  253.6 31.4 %copy-start.13 = (f32[256,768]{1,0:T(8,128)S(1)}, f32[256,768]{1,0:T(8,128)}, u32[]{:S(2)}) copy-start(f32[256,768]{1,0:T(8,128)} %copy-done.12) | copy-start | bytes 2359300
  253.6 72.1 %copy-start.42 = (bf16[256,768]{1,0:T(8,128)(2,1)S(1)}, bf16[256,768]{1,0:T(8,128)(2,1)}, u32[]{:S(2)}) copy-start(bf16[256,768]{1,0:T(8,128)(2,1)} %param.39) | copy-start | bytes 1179652
  253.6 149.5 %reduce-scatter.16.cloned.1.call-start = ((), (), s32[]{:S(2)}) async-start(), calls=%async_computation.15 | async-start | bytes 3932160 | tf_op jit(solution)/shard_map/reduce_scatter | solution.py:95
  328.4 10.8 %collective-permute-start.3 = (bf16[256,768]{1,0:T(8,128)(2,1)S(1)}, bf16[256,768]{1,0:T(8,128)(2,1)S(1)}, u32[]{:S(2)}, u32[]{:S(2)}) collective-permute-start(bf16[256,768]{1,0:T(8,128)(2,1)S(1)} %get-tuple-element.42), channel_id=1, source_target_pairs={{0,1},{1,2},{2,3},{3,0},{4,5},{5,6},{6,7},{7,4},{8,9},{9,10},{10,1... | collective-permute-start | bytes 1179656 | tf_op jit(solution)/shard_map/ppermute | solution.py:33
  328.4 10.8 %collective-permute-start.5 = (bf16[256,768]{1,0:T(8,128)(2,1)S(1)}, bf16[256,768]{1,0:T(8,128)(2,1)S(1)}, u32[]{:S(2)}, u32[]{:S(2)}) collective-permute-start(bf16[256,768]{1,0:T(8,128)(2,1)S(1)} %get-tuple-element.42), channel_id=1, source_target_pairs={{1,0},{2,1},{3,2},{0,3},{5,4},{6,5},{7,6},{4,7},{9,8},{10,9},{11,1... | collective-permute-start | bytes 1179656 | tf_op jit(solution)/shard_map/ppermute | solution.py:37
  339.3 7.2 collective-permute-start.4
  353.4 5.9 slice-start
  353.5 5.8 slice-start.1
  365.3 101.7 %reduce-scatter.20.cloned.1.call-start = ((), (), s32[]{:S(2)}) async-start(), calls=%async_computation.17 | async-start | bytes 7864320 | tf_op jit(solution)/shard_map/reduce_scatter | solution.py:250
  381.8 21.4 %copy-start.80 = (f32[768]{0:T(1024)S(1)}, f32[768]{0:T(1024)}, u32[]{:S(2)}) copy-start(f32[768]{0:T(1024)} %param.31) | copy-start | bytes 9220
  381.8 21.4 %copy-start.86 = (f32[256]{0:T(256)S(1)}, f32[256]{0:T(256)}, u32[]{:S(2)}) copy-start(f32[256]{0:T(256)} %copy-done.85) | copy-start | bytes 3076
  381.8 23.4 %copy-start.36 = (f32[256,768]{1,0:T(8,128)S(1)}, f32[256,768]{1,0:T(8,128)}, u32[]{:S(2)}) copy-start(f32[256,768]{1,0:T(8,128)} %get-tuple-element.43) | copy-start | bytes 2359300
  381.8 122.9 %reduce-scatter.18.cloned.1.call-start = ((), (), s32[]{:S(2)}) async-start(), calls=%async_computation.16 | async-start | bytes 3932160 | tf_op jit(solution)/shard_map/reduce_scatter | solution.py:95
  407.0 10.9 %collective-permute-start.6 = (bf16[256,768]{1,0:T(8,128)(2,1)S(1)}, bf16[256,768]{1,0:T(8,128)(2,1)S(1)}, u32[]{:S(2)}, u32[]{:S(2)}) collective-permute-start(bf16[256,768]{1,0:T(8,128)(2,1)S(1)} %get-tuple-element.40), channel_id=1, source_target_pairs={{0,1},{1,2},{2,3},{3,0},{4,5},{5,6},{6,7},{7,4},{8,9},{9,10},{10,1... | collective-permute-start | bytes 1179656 | tf_op jit(solution)/shard_map/ppermute | solution.py:33
  407.0 10.9 %collective-permute-start.8 = (bf16[256,768]{1,0:T(8,128)(2,1)S(1)}, bf16[256,768]{1,0:T(8,128)(2,1)S(1)}, u32[]{:S(2)}, u32[]{:S(2)}) collective-permute-start(bf16[256,768]{1,0:T(8,128)(2,1)S(1)} %get-tuple-element.40), channel_id=1, source_target_pairs={{1,0},{2,1},{3,2},{0,3},{5,4},{6,5},{7,6},{4,7},{9,8},{10,9},{11,1... | collective-permute-start | bytes 1179656 | tf_op jit(solution)/shard_map/ppermute | solution.py:37
  417.9 7.2 collective-permute-start.7
  441.3 377.5 %all-reduce.5.cloned.1.call-start = ((), (), s32[]{:S(2)}) async-start(), calls=%async_computation.18 | async-start | bytes 18874368 | tf_op jit(solution)/shard_map/psum | solution.py:279
  441.6 4.9 copy-start.44
  441.6 13.3 %slice-start.2 = ((s8[6291456]{0:T(1024)(128)(4,1)}), s8[4194304]{0:T(1024)(128)(4,1)S(1)}, s32[]{:S(2)}) async-start(s8[6291456]{0:T(1024)(128)(4,1)} %bitcast.258), calls=%async_computation.21 | async-start | bytes 8388608
  446.5 5.4 copy-start.10
  446.5 5.4 copy-start.27
  446.5 8.4 slice-start.3
  466.9 37.8 %copy-start.14 = (bf16[256,768]{1,0:T(8,128)(2,1)S(1)}, bf16[256,768]{1,0:T(8,128)(2,1)}, u32[]{:S(2)}) copy-start(bf16[256,768]{1,0:T(8,128)(2,1)} %param.20) | copy-start | bytes 1179652
  466.9 37.8 %copy-start.79 = (f32[768]{0:T(1024)S(1)}, f32[768]{0:T(1024)}, u32[]{:S(2)}) copy-start(f32[768]{0:T(1024)} %param.25) | copy-start | bytes 9220
  466.9 37.8 %copy-start.82 = (f32[256]{0:T(256)S(1)}, f32[256]{0:T(256)}, u32[]{:S(2)}) copy-start(f32[256]{0:T(256)} %copy-done.81) | copy-start | bytes 3076
  466.9 39.3 %copy-start.83 = (f32[768]{0:T(1024)S(1)}, f32[768]{0:T(1024)}, u32[]{:S(2)}) copy-start(f32[768]{0:T(1024)} %get-tuple-element.17) | copy-start | bytes 9220
  466.9 39.2 %copy-start.84 = (f32[768]{0:T(1024)S(1)}, f32[768]{0:T(1024)}, u32[]{:S(2)}) copy-start(f32[768]{0:T(1024)} %get-tuple-element.19) | copy-start | bytes 9220
  466.9 89.1 %copy-start.88 = (f32[256]{0:T(256)S(1)}, f32[256]{0:T(256)}, u32[]{:S(2)}) copy-start(f32[256]{0:T(256)} %get-tuple-element.51) | copy-start | bytes 3076
  466.9 89.1 %copy-start.39 = (f32[256,768]{1,0:T(8,128)S(1)}, f32[256,768]{1,0:T(8,128)}, u32[]{:S(2)}) copy-start(f32[256,768]{1,0:T(8,128)} %get-tuple-element.41) | copy-start | bytes 2359300
  504.7 51.4 %copy-start.37 = (f32[256,768]{1,0:T(8,128)S(1)}, f32[256,768]{1,0:T(8,128)}, u32[]{:S(2)}) copy-start(f32[256,768]{1,0:T(8,128)} %reduce-scatter.18.cloned.1.call-done) | copy-start | bytes 2359300
  (74 other events, 145.2 us)
Sparse Core Ops, SparseCore 0:
  11.2 22.3 all-gather.4
  43.1 37.9 reduce-scatter.7
  82.7 46.3 all-gather.6
  131.2 19.6 all-gather.8
  163.5 37.9 reduce-scatter.9
  205.1 23.6 all-gather.10
  247.0 37.9 reduce-scatter.13
  287.7 37.9 reduce-scatter.11
  365.4 37.6 reduce-scatter.15
  405.7 58.3 reduce-scatter.19
  466.6 37.9 reduce-scatter.17
  513.5 305.2 all-reduce.4
